TPU v7x, 32 devices: a whole 2x2x4 slice. The times are simulated.
32 devices in a mesh: row: 8 (over y, x, core), col: 4 (over z).
Axes of the slice: x: 2, y: 2, z: 4, core: 2. Of those that a mesh axis runs over, the one named last changes fastest.
Arguments:
- adjacency: int32 [2560, 80], P('row', 'col'), may hold values from -2147483648 to 2147483647, as said below
- relabel: int32 [2560], P(('row', 'col')), may hold values from 0 to 2559, each once
Outputs:
- clustering: float32 [2560], P(('row', 'col'))
- transitivity: float32 [], replicated
Inputs may be any that keep to these rules, and one draw needn't show every extreme that they name: The unpacked adjacency is symmetric with a zero diagonal.
All inputs are finite; a program needn't handle non-finite values.
Results may differ from a plain program's by a relative error of at most 0.0003.
Values sent between devices are 32-bit elements.
A program may use at most 128 MiB of HBM per device.

v0:
```python
import jax
import jax.numpy as jnp
from jax import lax
from jax.sharding import PartitionSpec as P


def unpack(words):
    shifts = jnp.arange(32, dtype=jnp.int32)
    bits = lax.shift_right_logical(words[:, :, None], shifts[None, None, :]) & 1
    return bits.reshape(words.shape[0], words.shape[1] * 32).astype(jnp.bfloat16)


def body(adjacency, relabel):
    local = unpack(adjacency)
    row_block = unpack(lax.all_gather(adjacency, "col", axis=1, tiled=True))
    paths = jnp.dot(
        row_block,
        unpack(lax.all_gather(adjacency, "row", axis=0, tiled=True)),
        preferred_element_type=jnp.float32,
    )
    wide = local.astype(jnp.float32)
    partial_value = jnp.sum(wide * paths, axis=1)
    degree_part = jnp.sum(wide, axis=1)
    closed, degree = (
        lax.psum_scatter(partial_value, "col", scatter_dimension=0, tiled=True),
        lax.psum_scatter(degree_part, "col", scatter_dimension=0, tiled=True),
    )
    wedges = jnp.maximum(degree * (degree - 1.0), 1.0)
    everyone = lax.all_gather(closed / wedges, ("row", "col"), axis=0, tiled=True)
    clustering = jnp.take(everyone, relabel, axis=0)
    sum_closed, sum_wedges = lax.psum((jnp.sum(closed), jnp.sum(wedges)), ("row", "col"))
    transitivity = sum_closed / sum_wedges
    return (clustering, transitivity)


def solution(mesh):
    placed = (P("row", "col"), P(("row", "col")))
    return jax.shard_map(
        body, mesh=mesh, in_specs=placed, out_specs=(P(("row", "col")), P()), check_vma=False
    )
```

profile of v0, /device:TPU:0, one launch (start us, length us, event | category | flops | bytes accessed | tf_op | source)
XLA Modules:
  0.0 88.2 jit_solution(8971569587029092777)
XLA Ops:
  0.6 1.2 %dynamic-slice = u32[1]{0:T(128)} dynamic-slice(u32[32]{0:T(128)} %constant.33, u32[]{:T(128)S(6)} %add.22), dynamic_slice_sizes={1} | dynamic-slice | bytes 12
  2.5 0.7 compare_select_fusion
  3.2 1.0 %convert_reduce_fusion = f32[320]{0:T(512)S(1)} fusion(s32[320,20]{0,1:T(8,128)} %param.2), kind=kLoop, calls=%fused_computation.5 | loop fusion | flops 1023680 | bytes 26880 | tf_op jit(solution)/shard_map/reduce_sum | solution.py:23
  4.2 0.1 shift_right_logical.70
  4.2 15.4 %all-gather = s32[4,20,320]{2,1,0:T(8,128)S(1)} all-gather(s32[1,20,320]{2,1,0:T(8,128)} %bitcast.16), channel_id=1, replica_groups=mesh['row'=8,'col'=4] {'col'}, dimensions={0}, use_global_device_ids=true | all-gather | bytes 128000 | tf_op jit(solution)/shard_map/all_gather | solution.py:15
  19.6 9.7 %all-gather.1 = s32[8,320,20]{1,2,0:T(8,128)S(1)} all-gather(s32[1,320,20]{1,2,0:T(8,128)} %bitcast.17), channel_id=1, replica_groups=mesh['row'=8,'col'=4] {'row'}, dimensions={0}, use_global_device_ids=true | all-gather | bytes 230400 | tf_op jit(solution)/shard_map/all_gather | solution.py:18
  29.4 0.1 reshape.100
  29.5 0.8 shift_right_logical.67
  30.3 0.3 copy.8
  30.6 0.7 and_convert_fusion.1
  31.3 0.9 %and_convert_fusion = bf16[2560,20,32]{0,2,1:T(8,128)(2,1)S(1)} fusion(s32[2560,20]{0,1:T(8,128)S(1)} %reshape.100), kind=kLoop, calls=%fused_computation.1 | loop fusion | flops 4915200 | bytes 3481600 | tf_op jit(solution)/shard_map/convert_element_type | solution.py:10
  32.2 0.0 copy-start
  32.2 1.8 %fusion = f32[320]{0:T(512)S(1)} fusion(bf16[320,2560]{0,1:T(8,128)(2,1)S(1)} %bitcast.15, bf16[2560,640]{0,1:T(8,128)(2,1)S(1)} %bitcast.14, s32[320,640]{1,0:T(8,128)S(1)} %copy.8, s32[640]{0:T(1024)S(1)} %shift_right_logical.70), kind=kOutput, calls=%fused_computation.4 | convolution fusion | flops 1049804480 | bytes 5738240 | tf_op jit(solution)/shard_map/dot_general | solution.py:16
  34.1 12.1 %all-reduce.4 = (f32[320]{0:T(512)S(1)}, f32[320]{0:T(512)S(1)}) all-reduce(f32[320]{0:T(512)S(1)} %fusion, f32[320]{0:T(512)S(1)} %convert_reduce_fusion), channel_id=2, replica_groups=mesh['row'=8,'col'=4] {'col'}, use_global_device_ids=true, to_apply=%region_1.0.clone | all-reduce | flops 640 | bytes 5120
  46.2 0.8 fusion.2
  46.9 37.1 %all-reduce.3 = (f32[2560]{0:T(1024)S(1)}, f32[]{:T(128)}, f32[]{:T(128)}) all-reduce(f32[2560]{0:T(1024)S(1)} %get-tuple-element.8, f32[]{:T(128)} %get-tuple-element.9, f32[]{:T(128)} %get-tuple-element.7), channel_id=1, replica_groups=mesh['row'=8,'col'=4] {'row','col'}, use_global_device_ids=true, to_apply=%add | all-reduce | flops 2562 | bytes 20496
  85.4 1.1 %gather_fusion = f32[80]{0:T(128)S(1)} fusion(f32[2560]{0:T(1024)S(1)} %get-tuple-element.2, s32[1024]{0:T(1024)S(1)} %pad_clamp_fusion), kind=kCustom, calls=%fused_computation | custom fusion | bytes 960 | tf_op jit(solution)/shard_map/jit(_take)/gather | solution.py:30
  86.5 0.0 copy-done
  86.5 0.5 and_select_fusion
  (5 shorter events, 0.1 us)
Async XLA Ops:
  32.2 54.3 %copy-start = (s32[80]{0:T(128)S(1)}, s32[80]{0:T(128)}, u32[]{:S(2)}) copy-start(s32[80]{0:T(128)} %param.3) | copy-start | bytes 964
where the time goes:
time: 89.7 us; the launch traced here: 88.2 us
  blocking collectives  74.2 us (83%)
  other arithmetic  4.52 us (5%)
  between operations  3.83 us (4%)
  local copies, waits for them, and re-layouts  3.79 us (4%)
  matrix products  1.85 us (2%)
    unnamed x2, blocking collectives  49.1 us
    all_gather x1, blocking collectives, body(): row_block = unpack(lax.all_gather(adjacency, 'col', axis=1, tiled=True))  15.4 us
    all_gather x1, blocking collectives, body(): lax.all_gather(adjacency, 'row', axis=0, tiled=True)  9.67 us
    dot_general x1, matrix products, body(): jnp.dot(row_block, unpack(lax.all_gather(adjacency, 'row', axis=0, tiled=...  1.85 us

commit v1 on v0

v1 whole, which is shorter than its diff:
```python
import functools

import jax
import jax.numpy as jnp
from jax import lax
from jax.experimental import pallas as pl
from jax.experimental.pallas import tpu as pltpu
from jax.sharding import PartitionSpec as P

MESH = pl.DeviceIdType.MESH
TYPE = jnp.float8_e4m3fn


def unpack(row):
    wide = jnp.broadcast_to(row, (32, row.shape[1]))
    bits = lax.shift_right_logical(wide, lax.broadcasted_iota(jnp.int32, wide.shape, 0)) & 1
    return bits.astype(jnp.float32).astype(TYPE)


def kernel(
    n_row, n_col, words_ref, relabel_ref, out_ref, total_ref,
    xs, ys, yw, x, y, hot, rel, msg,
    x_send, x_recv, y_send, y_recv, m_send, m_recv, local_sem,
):
    n_words, n_rows = words_ref.shape
    n_mine = relabel_ref.shape[1]
    depth = 32 * n_words
    width = msg.shape[1]
    r, c = lax.axis_index("row"), lax.axis_index("col")
    barrier = pltpu.get_barrier_semaphore()
    col_peers = [lax.rem(c + o, n_col) for o in range(1, n_col)]
    row_peers = [lax.rem(r + o, n_row) for o in range(1, n_row)]
    for p in col_peers:
        pl.semaphore_signal(barrier, inc=1, device_id=(r, p), device_id_type=MESH)
    for p in row_peers:
        pl.semaphore_signal(barrier, inc=1, device_id=(p, c), device_id_type=MESH)
    load_x = pltpu.make_async_copy(words_ref, xs.at[c], local_sem.at[0])
    load_y = pltpu.make_async_copy(words_ref, ys.at[r], local_sem.at[1])
    load_r = pltpu.make_async_copy(relabel_ref, rel, local_sem.at[2])
    load_x.start()
    load_y.start()
    load_r.start()
    load_x.wait()
    load_y.wait()
    pl.semaphore_wait(barrier, n_col + n_row - 2)

    sends = []
    for i, p in enumerate(col_peers):
        sends.append(pltpu.make_async_remote_copy(
            xs.at[c], xs.at[c], x_send.at[i], x_recv.at[c], device_id=(r, p), device_id_type=MESH))
    for i, p in enumerate(row_peers):
        sends.append(pltpu.make_async_remote_copy(
            ys.at[r], ys.at[r], y_send.at[i], y_recv.at[r], device_id=(p, c), device_id_type=MESH))
    for copy in sends:
        copy.start()

    load_r.wait()
    label = rel[...]
    owner = jnp.zeros_like(label)
    for k in range(1, n_row):
        owner += (label >= k * n_rows).astype(jnp.int32)
    place = label - owner * n_rows
    hot[...] = (lax.broadcasted_iota(jnp.int32, hot.shape, 0) == place).astype(jnp.float32).astype(jnp.bfloat16)
    y[depth:, :] = jnp.ones((y.shape[0] - depth, y.shape[1]), TYPE)

    def take_x(block):
        def one(w, carry):
            start = pl.multiple_of(block * depth + w * 32, 32)
            x[pl.ds(start, 32), :] = unpack(xs[block, pl.ds(w, 1), :])
            return carry
        lax.fori_loop(0, n_words, one, 0, unroll=4)

    take_x(c)
    for i, p in enumerate(col_peers):
        pltpu.make_async_remote_copy(
            xs.at[p], xs.at[p], x_send.at[i], x_recv.at[p], device_id=(r, p), device_id_type=MESH).wait_recv()
        take_x(p)
    for i, p in enumerate(row_peers):
        pltpu.make_async_remote_copy(
            ys.at[p], ys.at[p], y_send.at[i], y_recv.at[p], device_id=(p, c), device_id_type=MESH).wait_recv()
    yw[...] = jnp.concatenate([ys[k] for k in range(n_row)], axis=1)

    def one_y(w, carry):
        y[pl.ds(pl.multiple_of(w * 32, 32), 32), :] = unpack(yw[pl.ds(w, 1), :])
        return carry
    lax.fori_loop(0, n_words, one_y, 0, unroll=2)

    paths = jnp.dot(y[...], x[...], preferred_element_type=jnp.float32)
    mask = x[pl.ds(pl.multiple_of(c * depth, 32), depth), :].astype(jnp.float32)
    closed = jnp.sum(paths[:depth] * mask, axis=0, keepdims=True)
    degree = paths[depth : depth + 1]
    wedges = jnp.maximum(degree * (degree - 1.0), 1.0)
    sums = lax.broadcasted_iota(jnp.int32, (1, width - n_rows), 1)
    tail = jnp.where(sums == 0, jnp.sum(closed), jnp.where(sums == 1, jnp.sum(wedges), 0.0))
    me = c * n_row + r
    msg[pl.ds(me, 1), :] = jnp.concatenate([closed / wedges, tail], axis=1)

    posts = []
    i = 0
    for oc in reversed(range(n_col)):
        for orow in range(n_row):
            if oc == 0 and orow == 0:
                continue
            posts.append(pltpu.make_async_remote_copy(
                msg.at[pl.ds(me, 1)], msg.at[pl.ds(me, 1)], m_send.at[i], m_recv.at[me],
                device_id=(lax.rem(r + orow, n_row), lax.rem(c + oc, n_col)), device_id_type=MESH))
            i += 1
    for copy in posts:
        copy.start()
    for copy in sends:
        copy.wait_send()
    for o in range(1, n_row * n_col):
        p = lax.rem(me + o, n_row * n_col)
        pltpu.make_async_copy(msg.at[pl.ds(p, 1)], msg.at[pl.ds(p, 1)], m_recv.at[p]).wait()

    ratio = msg[0:n_row, :]
    for k in range(1, n_col):
        ratio += msg[k * n_row : (k + 1) * n_row, :]
    high = ratio.astype(jnp.bfloat16)
    rest = ratio - high.astype(jnp.float32)
    middle = rest.astype(jnp.bfloat16)
    low = (rest - middle.astype(jnp.float32)).astype(jnp.bfloat16)
    found = jnp.zeros((n_row, n_mine), jnp.float32)
    for part in (high, middle, low):
        found += jnp.dot(part, hot[...], preferred_element_type=jnp.float32)
    which = lax.broadcasted_iota(jnp.int32, found.shape, 0)
    out_ref[...] = jnp.sum(jnp.where(which == owner, found, 0.0), axis=0, keepdims=True)
    sum_closed = jnp.sum(ratio[:, n_rows : n_rows + 1], axis=0, keepdims=True)
    sum_wedges = jnp.sum(ratio[:, n_rows + 1 : n_rows + 2], axis=0, keepdims=True)
    total_ref[...] = sum_closed / (sum_wedges * (1.0 / n_col))
    for copy in posts:
        copy.wait_send()


def solution(mesh):
    n_row, n_col = mesh.shape["row"], mesh.shape["col"]
    n_all = n_row * n_col

    def body(adjacency, relabel):
        n_rows, n_words = adjacency.shape
        n_mine = relabel.shape[0]
        depth = 32 * n_words
        every = n_row * n_rows
        width = (n_rows + 2 + 127) // 128 * 128
        clustering, total = pl.pallas_call(
            functools.partial(kernel, n_row, n_col),
            out_shape=(
                jax.ShapeDtypeStruct((1, n_mine), jnp.float32),
                jax.ShapeDtypeStruct((1, 1), jnp.float32),
            ),
            in_specs=[pl.BlockSpec(memory_space=pl.ANY)] * 2,
            out_specs=[pl.BlockSpec(memory_space=pltpu.VMEM)] * 2,
            scratch_shapes=[
                pltpu.VMEM((n_col, n_words, n_rows), jnp.int32),
                pltpu.VMEM((n_row, n_words, n_rows), jnp.int32),
                pltpu.VMEM((n_words, every), jnp.int32),
                pltpu.VMEM((every, n_rows), TYPE),
                pltpu.VMEM((depth + 32, every), TYPE),
                pltpu.VMEM((width, n_mine), jnp.bfloat16),
                pltpu.VMEM((1, n_mine), jnp.int32),
                pltpu.VMEM((n_all, width), jnp.float32),
                pltpu.SemaphoreType.DMA((n_col - 1,)),
                pltpu.SemaphoreType.DMA((n_col,)),
                pltpu.SemaphoreType.DMA((n_row - 1,)),
                pltpu.SemaphoreType.DMA((n_row,)),
                pltpu.SemaphoreType.DMA((n_all - 1,)),
                pltpu.SemaphoreType.DMA((n_all,)),
                pltpu.SemaphoreType.DMA((3,)),
            ],
            compiler_params=pltpu.CompilerParams(
                collective_id=0, has_side_effects=True, vmem_limit_bytes=64000 * 1024
            ),
        )(adjacency.T, relabel.reshape(1, n_mine))
        return clustering.reshape(n_mine), total.reshape(())

    placed = (P("row", "col"), P(("row", "col")))
    return jax.shard_map(
        body, mesh=mesh, in_specs=placed, out_specs=(P(("row", "col")), P()), check_vma=False
    )
```

time: 89.7 us -> 23.8 us (0.27); the launches traced: 88.2 us -> 23.6 us
  blocking collectives: 74.2 us -> 0 us
  Pallas kernels: 0 us -> 20.1 us
  other arithmetic: 4.52 us -> 0 us
  local copies, waits for them, and re-layouts: 3.79 us -> 1.13 us
  matrix products: 1.85 us -> 0 us
  between operations: 3.83 us -> 2.41 us
    unnamed x2 -> x0, blocking collectives: 49.1 us -> none
    all_gather x2 -> x0, blocking collectives: 25.1 us -> none  [the longest x1 15.4 us: body(): row_block = unpack(lax.all_gather(adjacency, 'col', axis=1, tiled=True))]
    pallas_call x0 -> x1, Pallas kernels: none -> 20.1 us  [body(): pl.pallas_call(functools.partial(kernel, n_row, n_col), out_shape=(jax.Sh...]
    dot_general x1 -> x0, matrix products: 1.85 us -> none  [body(): jnp.dot(row_block, unpack(lax.all_gather(adjacency, 'row', axis=0, tiled=...]
    reduce_sum x2 -> x0, other arithmetic: 1.75 us -> none  [the longest x1 0.95 us: body(): degree_part = jnp.sum(wide, axis=1)]
    convert_element_type x2 -> x0, other arithmetic: 1.59 us -> none  [unpack(): bits.reshape(words.shape[0], words.shape[1] * 32).astype(jnp.bfloat16)]
    shift_right_logical x4 -> x0, local copies, waits for them, and re-layouts: 1.22 us -> none  [unpack(): bits = lax.shift_right_logical(words[:, :, None], shifts[None, None, :]) & 1]
    select_n x2 -> x0, other arithmetic: 1.18 us -> none  [body(): clustering = jnp.take(everyone, relabel, axis=0)]
where the time goes in v1:
time: 23.8 us; the launch traced here: 23.6 us
  Pallas kernels  20.1 us (84%)
  between operations  2.41 us (10%)
  local copies, waits for them, and re-layouts  1.13 us (5%)
    pallas_call x1, Pallas kernels, body(): pl.pallas_call(functools.partial(kernel, n_row, n_col), out_shape=(jax.Sh...  20.1 us
    unnamed x3, local copies, waits for them, and re-layouts  1.13 us

profile of v1, /device:TPU:0, one launch (start us, length us, event | category | flops | bytes accessed | tf_op | source)
XLA Modules:
  0.0 23.6 jit_solution(8915798980685048539)
XLA Ops:
  0.6 20.1 %shard_map.41 = (f32[1,80]{1,0:T(1,128)}, f32[1,1]{1,0:T(1,128)}) custom-call(s32[20,320]{1,0:T(8,128)} %bitcast.4, s32[1,80]{1,0:T(1,128)} %bitcast.5), custom_call_target="tpu_custom_call" | custom-call | tf_op jit(solution)/shard_map/pallas_call | solution.py:145
  20.7 0.0 copy-start
  20.7 0.6 %copy-done = f32[1,80]{1,0:T(1,128)S(1)} copy-done((f32[1,80]{1,0:T(1,128)S(1)}, f32[1,80]{1,0:T(1,128)}, u32[]{:S(2)}) %copy-start) | copy-done | bytes 344
  21.3 0.5 %copy.6 = f32[80]{0:T(128)} copy(f32[80]{0:T(128)S(1)} %bitcast.6) | data formatting | bytes 640
Async XLA Ops:
  20.7 0.6 %copy-start = (f32[1,80]{1,0:T(1,128)S(1)}, f32[1,80]{1,0:T(1,128)}, u32[]{:S(2)}) copy-start(f32[1,80]{1,0:T(1,128)} %get-tuple-element.4) | copy-start | bytes 964

commit v2 on v1

--- a/solution.py
+++ b/solution.py
@@ -20,7 +20,7 @@
 def kernel(
     n_row, n_col, words_ref, relabel_ref, out_ref, total_ref,
     xs, ys, yw, x, y, hot, rel, msg,
-    x_send, x_recv, y_send, y_recv, m_send, m_recv, local_sem,
+    x_send, x_recv, y_send, y_recv, m_send, m_recv, local_sem, ready, plane,
 ):
     n_words, n_rows = words_ref.shape
     n_mine = relabel_ref.shape[1]
@@ -28,31 +28,48 @@
     width = msg.shape[1]
     r, c = lax.axis_index("row"), lax.axis_index("col")
     barrier = pltpu.get_barrier_semaphore()
-    col_peers = [lax.rem(c + o, n_col) for o in range(1, n_col)]
-    row_peers = [lax.rem(r + o, n_row) for o in range(1, n_row)]
-    for p in col_peers:
-        pl.semaphore_signal(barrier, inc=1, device_id=(r, p), device_id_type=MESH)
-    for p in row_peers:
-        pl.semaphore_signal(barrier, inc=1, device_id=(p, c), device_id_type=MESH)
+
+    def each_col(do, when):
+        for p in range(n_col):
+            pl.when(when(p, c))(functools.partial(do, p))
+
+    def each_row(do, when):
+        for p in range(n_row):
+            pl.when(when(p, r))(functools.partial(do, p))
+
+    above, below, other = (lambda p, q: p > q), (lambda p, q: p < q), (lambda p, q: p != q)
+
+    def tell(sem, device):
+        pl.semaphore_signal(sem, inc=1, device_id=device, device_id_type=MESH)
+
+    each_col(lambda p: tell(barrier, (r, p)), above)
+    each_row(lambda p: tell(barrier, (p, c)), above)
     load_x = pltpu.make_async_copy(words_ref, xs.at[c], local_sem.at[0])
     load_y = pltpu.make_async_copy(words_ref, ys.at[r], local_sem.at[1])
     load_r = pltpu.make_async_copy(relabel_ref, rel, local_sem.at[2])
     load_x.start()
     load_y.start()
     load_r.start()
+
+    @pl.when(c + r > 0)
+    def _():
+        pl.semaphore_wait(barrier, c + r)
+
+    each_col(lambda p: tell(ready.at[c], (r, p)), below)
+    each_row(lambda p: tell(ready.at[n_col + r], (p, c)), below)
+
+    def post_x(p):
+        return pltpu.make_async_remote_copy(
+            xs.at[c], xs.at[c], x_send.at[p], x_recv.at[c], device_id=(r, p), device_id_type=MESH)
+
+    def post_y(p):
+        return pltpu.make_async_remote_copy(
+            ys.at[r], ys.at[r], y_send.at[p], y_recv.at[r], device_id=(p, c), device_id_type=MESH)
+
     load_x.wait()
+    each_col(lambda p: post_x(p).start(), below)
     load_y.wait()
-    pl.semaphore_wait(barrier, n_col + n_row - 2)
-
-    sends = []
-    for i, p in enumerate(col_peers):
-        sends.append(pltpu.make_async_remote_copy(
-            xs.at[c], xs.at[c], x_send.at[i], x_recv.at[c], device_id=(r, p), device_id_type=MESH))
-    for i, p in enumerate(row_peers):
-        sends.append(pltpu.make_async_remote_copy(
-            ys.at[r], ys.at[r], y_send.at[i], y_recv.at[r], device_id=(p, c), device_id_type=MESH))
-    for copy in sends:
-        copy.start()
+    each_row(lambda p: post_y(p).start(), below)
 
     load_r.wait()
     label = rel[...]
@@ -71,13 +88,26 @@
         lax.fori_loop(0, n_words, one, 0, unroll=4)
 
     take_x(c)
-    for i, p in enumerate(col_peers):
-        pltpu.make_async_remote_copy(
-            xs.at[p], xs.at[p], x_send.at[i], x_recv.at[p], device_id=(r, p), device_id_type=MESH).wait_recv()
+
+    def up_x(p):
+        pl.semaphore_wait(ready.at[p], 1)
+        post_x(p).start()
+
+    def up_y(p):
+        pl.semaphore_wait(ready.at[n_col + p], 1)
+        post_y(p).start()
+
+    each_col(up_x, above)
+    each_row(up_y, above)
+    each_col(lambda p: tell(plane, (r, p)), other)
+
+    for o in range(1, n_col):
+        p = lax.rem(c + o, n_col)
+        pltpu.make_async_copy(xs.at[p], xs.at[p], x_recv.at[p]).wait()
         take_x(p)
-    for i, p in enumerate(row_peers):
-        pltpu.make_async_remote_copy(
-            ys.at[p], ys.at[p], y_send.at[i], y_recv.at[p], device_id=(p, c), device_id_type=MESH).wait_recv()
+    for o in range(1, n_row):
+        p = lax.rem(r + o, n_row)
+        pltpu.make_async_copy(ys.at[p], ys.at[p], y_recv.at[p]).wait()
     yw[...] = jnp.concatenate([ys[k] for k in range(n_row)], axis=1)
 
     def one_y(w, carry):
@@ -105,10 +135,11 @@
                 msg.at[pl.ds(me, 1)], msg.at[pl.ds(me, 1)], m_send.at[i], m_recv.at[me],
                 device_id=(lax.rem(r + orow, n_row), lax.rem(c + oc, n_col)), device_id_type=MESH))
             i += 1
+    pl.semaphore_wait(plane, n_col - 1)
     for copy in posts:
         copy.start()
-    for copy in sends:
-        copy.wait_send()
+    each_col(lambda p: post_x(p).wait_send(), other)
+    each_row(lambda p: post_y(p).wait_send(), other)
     for o in range(1, n_row * n_col):
         p = lax.rem(me + o, n_row * n_col)
         pltpu.make_async_copy(msg.at[pl.ds(p, 1)], msg.at[pl.ds(p, 1)], m_recv.at[p]).wait()
@@ -159,13 +190,15 @@
                 pltpu.VMEM((width, n_mine), jnp.bfloat16),
                 pltpu.VMEM((1, n_mine), jnp.int32),
                 pltpu.VMEM((n_all, width), jnp.float32),
-                pltpu.SemaphoreType.DMA((n_col - 1,)),
                 pltpu.SemaphoreType.DMA((n_col,)),
-                pltpu.SemaphoreType.DMA((n_row - 1,)),
+                pltpu.SemaphoreType.DMA((n_col,)),
+                pltpu.SemaphoreType.DMA((n_row,)),
                 pltpu.SemaphoreType.DMA((n_row,)),
                 pltpu.SemaphoreType.DMA((n_all - 1,)),
                 pltpu.SemaphoreType.DMA((n_all,)),
                 pltpu.SemaphoreType.DMA((3,)),
+                pltpu.SemaphoreType.REGULAR((n_col + n_row,)),
+                pltpu.SemaphoreType.REGULAR,
             ],
             compiler_params=pltpu.CompilerParams(
                 collective_id=0, has_side_effects=True, vmem_limit_bytes=64000 * 1024

time: 23.8 us -> 23.9 us (level)
  no operation moved by 1% of the time
where the time goes in v2:
time: 23.9 us; the launch traced here: 23.7 us
  Pallas kernels  20.2 us (85%)
  between operations  2.41 us (10%)
  local copies, waits for them, and re-layouts  1.13 us (5%)
    pallas_call x1, Pallas kernels, body(): pl.pallas_call(functools.partial(kernel, n_row, n_col), out_shape=(jax.Sh...  20.2 us
    unnamed x3, local copies, waits for them, and re-layouts  1.13 us

profile of v2, /device:TPU:0, one launch (start us, length us, event | category | flops | bytes accessed | tf_op | source)
XLA Modules:
  0.0 23.7 jit_solution(18225655027745565001)
XLA Ops:
  0.6 20.2 %shard_map.41 = (f32[1,80]{1,0:T(1,128)}, f32[1,1]{1,0:T(1,128)}) custom-call(s32[20,320]{1,0:T(8,128)} %bitcast.4, s32[1,80]{1,0:T(1,128)} %bitcast.5), custom_call_target="tpu_custom_call" | custom-call | tf_op jit(solution)/shard_map/pallas_call | solution.py:176
  20.8 0.0 copy-start
  20.8 0.6 %copy-done = f32[1,80]{1,0:T(1,128)S(1)} copy-done((f32[1,80]{1,0:T(1,128)S(1)}, f32[1,80]{1,0:T(1,128)}, u32[]{:S(2)}) %copy-start) | copy-done | bytes 344
  21.4 0.5 %copy.6 = f32[80]{0:T(128)} copy(f32[80]{0:T(128)S(1)} %bitcast.6) | data formatting | bytes 640
Async XLA Ops:
  20.8 0.6 %copy-start = (f32[1,80]{1,0:T(1,128)S(1)}, f32[1,80]{1,0:T(1,128)}, u32[]{:S(2)}) copy-start(f32[1,80]{1,0:T(1,128)} %get-tuple-element.4) | copy-start | bytes 964

commit v3 on v1

--- a/solution.py
+++ b/solution.py
@@ -96,15 +96,11 @@
     msg[pl.ds(me, 1), :] = jnp.concatenate([closed / wedges, tail], axis=1)
 
     posts = []
-    i = 0
-    for oc in reversed(range(n_col)):
-        for orow in range(n_row):
-            if oc == 0 and orow == 0:
-                continue
-            posts.append(pltpu.make_async_remote_copy(
-                msg.at[pl.ds(me, 1)], msg.at[pl.ds(me, 1)], m_send.at[i], m_recv.at[me],
-                device_id=(lax.rem(r + orow, n_row), lax.rem(c + oc, n_col)), device_id_type=MESH))
-            i += 1
+    for i in range(n_row * n_col - 1):
+        to = i + (i >= me).astype(jnp.int32)
+        posts.append(pltpu.make_async_remote_copy(
+            msg.at[pl.ds(me, 1)], msg.at[pl.ds(me, 1)], m_send.at[i], m_recv.at[me],
+            device_id=(lax.rem(to, n_row), to // n_row), device_id_type=MESH))
     for copy in posts:
         copy.start()
     for copy in sends:

time: 23.8 us -> 23.5 us (0.987)
  Pallas kernels: 20.1 us -> 19.8 us
    pallas_call x1, Pallas kernels: 20.1 us -> 19.8 us  [body(): pl.pallas_call(functools.partial(kernel, n_row, n_col), out_shape=(jax.Sh...]
where the time goes in v3:
time: 23.5 us; the launch traced here: 23.3 us
  Pallas kernels  19.8 us (84%)
  between operations  2.41 us (10%)
  local copies, waits for them, and re-layouts  1.13 us (5%)
    pallas_call x1, Pallas kernels, body(): pl.pallas_call(functools.partial(kernel, n_row, n_col), out_shape=(jax.Sh...  19.8 us
    unnamed x3, local copies, waits for them, and re-layouts  1.13 us

profile of v3, /device:TPU:0, one launch (start us, length us, event | category | flops | bytes accessed | tf_op | source)
XLA Modules:
  0.0 23.3 jit_solution(13599750801823389443)
XLA Ops:
  0.6 19.8 %shard_map.41 = (f32[1,80]{1,0:T(1,128)}, f32[1,1]{1,0:T(1,128)}) custom-call(s32[20,320]{1,0:T(8,128)} %bitcast.4, s32[1,80]{1,0:T(1,128)} %bitcast.5), custom_call_target="tpu_custom_call" | custom-call | tf_op jit(solution)/shard_map/pallas_call | solution.py:141
  20.4 0.0 copy-start
  20.4 0.6 %copy-done = f32[1,80]{1,0:T(1,128)S(1)} copy-done((f32[1,80]{1,0:T(1,128)S(1)}, f32[1,80]{1,0:T(1,128)}, u32[]{:S(2)}) %copy-start) | copy-done | bytes 344
  21.0 0.5 %copy.6 = f32[80]{0:T(128)} copy(f32[80]{0:T(128)S(1)} %bitcast.6) | data formatting | bytes 640
Async XLA Ops:
  20.4 0.6 %copy-start = (f32[1,80]{1,0:T(1,128)S(1)}, f32[1,80]{1,0:T(1,128)}, u32[]{:S(2)}) copy-start(f32[1,80]{1,0:T(1,128)} %get-tuple-element.4) | copy-start | bytes 964

commit v4 on v3

--- a/solution.py
+++ b/solution.py
@@ -116,9 +116,9 @@
     rest = ratio - high.astype(jnp.float32)
     middle = rest.astype(jnp.bfloat16)
     low = (rest - middle.astype(jnp.float32)).astype(jnp.bfloat16)
-    found = jnp.zeros((n_row, n_mine), jnp.float32)
-    for part in (high, middle, low):
-        found += jnp.dot(part, hot[...], preferred_element_type=jnp.float32)
+    parts = jnp.concatenate([p.astype(jnp.float32) for p in (high, middle, low)], axis=0).astype(jnp.bfloat16)
+    picked = jnp.dot(parts, hot[...], preferred_element_type=jnp.float32)
+    found = picked[:n_row] + picked[n_row : 2 * n_row] + picked[2 * n_row :]
     which = lax.broadcasted_iota(jnp.int32, found.shape, 0)
     out_ref[...] = jnp.sum(jnp.where(which == owner, found, 0.0), axis=0, keepdims=True)
     sum_closed = jnp.sum(ratio[:, n_rows : n_rows + 1], axis=0, keepdims=True)

time: 23.5 us -> 23.5 us (level)
  no operation moved by 1% of the time
where the time goes in v4:
time: 23.5 us; the launch traced here: 23.3 us
  Pallas kernels  19.8 us (84%)
  between operations  2.41 us (10%)
  local copies, waits for them, and re-layouts  1.13 us (5%)
    pallas_call x1, Pallas kernels, body(): pl.pallas_call(functools.partial(kernel, n_row, n_col), out_shape=(jax.Sh...  19.8 us
    unnamed x3, local copies, waits for them, and re-layouts  1.13 us

profile of v4, /device:TPU:0, one launch (start us, length us, event | category | flops | bytes accessed | tf_op | source)
XLA Modules:
  0.0 23.3 jit_solution(15175682936962892431)
XLA Ops:
  0.6 19.8 %shard_map.41 = (f32[1,80]{1,0:T(1,128)}, f32[1,1]{1,0:T(1,128)}) custom-call(s32[20,320]{1,0:T(8,128)} %bitcast.4, s32[1,80]{1,0:T(1,128)} %bitcast.5), custom_call_target="tpu_custom_call" | custom-call | tf_op jit(solution)/shard_map/pallas_call | solution.py:141
  20.4 0.0 copy-start
  20.4 0.6 %copy-done = f32[1,80]{1,0:T(1,128)S(1)} copy-done((f32[1,80]{1,0:T(1,128)S(1)}, f32[1,80]{1,0:T(1,128)}, u32[]{:S(2)}) %copy-start) | copy-done | bytes 344
  21.0 0.5 %copy.6 = f32[80]{0:T(128)} copy(f32[80]{0:T(128)S(1)} %bitcast.6) | data formatting | bytes 640
Async XLA Ops:
  20.4 0.6 %copy-start = (f32[1,80]{1,0:T(1,128)S(1)}, f32[1,80]{1,0:T(1,128)}, u32[]{:S(2)}) copy-start(f32[1,80]{1,0:T(1,128)} %get-tuple-element.4) | copy-start | bytes 964
